TPU v7x, 32 devices: a whole 2x2x4 slice. The times are simulated.
32 devices in a mesh: ctx: 8 (over y, x, core), tp: 4 (over z).
Axes of the slice: x: 2, y: 2, z: 4, core: 2. Of those that a mesh axis runs over, the one named last changes fastest.
Arguments:
- hidden: bfloat16 [8, 8192], P(None, 'ctx'), may hold values from -4.8 to 4.8, as said below
- norm_gains: bfloat16 [4, 8192], P(None, 'ctx'), may hold values from 0.5 to 1.5
- w_query: bfloat16 [4, 8192, 8192], P(None, 'ctx', 'tp'), may hold values from -0.0625 to 0.0625
- w_key: bfloat16 [4, 8192, 1024], P(None, 'ctx', 'tp'), may hold values from -0.125 to 0.125
- w_value: bfloat16 [4, 8192, 1024], P(None, 'ctx', 'tp'), may hold values from -0.125 to 0.125
- w_out: bfloat16 [4, 8192, 8192], P(None, 'tp', 'ctx'), may hold values from -0.0625 to 0.0625
- key_cache: bfloat16 [4, 8, 8, 1024, 128], P(None, None, 'tp', 'ctx'), may hold values from -9 to 9
- value_cache: bfloat16 [4, 8, 8, 1024, 128], P(None, None, 'tp', 'ctx'), may hold values from -6 to 6
- lengths: int32 [8], replicated, may hold values from 1 to 1024, 4104 in all
Outputs:
- updated: float32 [8, 8192], P(None, 'ctx')
Inputs may be any that keep to these rules, and one draw needn't show every extreme that they name: Each sequence has lengths[b] valid cache positions 0 .. lengths[b] - 1, between 1 and 1024; the longest sequence has exactly 1024; the new token sits at position lengths[b]. `hidden`: activations of order 0.2; in each block of 1024 consecutive features one sequence, chosen at random, has entries four times larger.
All inputs are finite; a program needn't handle non-finite values.
Results may differ from a plain program's by a relative error of at most 0.02.
Values sent between devices are 32-bit elements.
A program may use at most 128 MiB of HBM per device.

v0:
```python
import math
import jax
import jax.numpy as jnp
from jax import lax
from jax.sharding import PartitionSpec as P

D = 8192
mask_fill = -1e30
norm_eps = 1e-05
rope_base = 500000.0


def merged(value, axis, join):
    pieces = jax.tree.map(lambda part: lax.all_gather(part, axis), value)
    head = jax.tree.map(lambda part: part[0], pieces)
    tail = jax.tree.map(lambda part: part[1:], pieces)
    total, _ = lax.scan(lambda total, slab: (join(total, slab), None), head, tail)
    return total


def rotate(vectors, positions):
    width = vectors.shape[-1]
    half_width = width // 2
    exponents = jnp.arange(half_width, dtype=jnp.float32) * (2.0 / width)
    frequency = jnp.exp(-exponents * math.log(rope_base))
    angles = positions.astype(jnp.float32)[:, None] * frequency[None, :]
    cosine = jnp.cos(angles)[:, None, :]
    sine_part = jnp.sin(angles)[:, None, :]
    first_half = vectors[..., :half_width]
    second_half = vectors[..., half_width:]
    return jnp.concatenate(
        [
            first_half * cosine - second_half * sine_part,
            second_half * cosine + first_half * sine_part,
        ],
        axis=-1,
    )


def combine_partial(one_side, other_side):
    first_max, first_sum, first_out = one_side
    second_max, second_sum, second_out = other_side
    largest = jnp.maximum(first_max, second_max)
    first_factor = jnp.exp(first_max - largest)
    second_factor = jnp.exp(second_max - largest)
    merged_sum = first_sum * first_factor + second_sum * second_factor
    merged_out = first_out * first_factor[..., None] + second_out * second_factor[..., None]
    return (largest, merged_sum, merged_out)


def shards(hidden, norm_gains, w_query, w_key, w_value, w_out, key_cache, value_cache, lengths):
    stream = hidden.astype(jnp.float32)
    seq_count = hidden.shape[0]
    head_width = key_cache.shape[4]
    location_total = key_cache.shape[3]
    kv_local = key_cache.shape[2]
    query_local = w_query.shape[2] // head_width
    group_size = query_local // kv_local
    logit_multiplier = 1.0 / math.sqrt(head_width)
    positions = lax.axis_index("ctx") * location_total + jnp.arange(location_total, dtype=jnp.int32)
    usable = (positions[None, :] < lengths[:, None])[:, None, None, :]
    for layer_idx in range(w_query.shape[0]):
        local_squares = jnp.sum(stream * stream, axis=1)
        scaled = (stream * norm_gains[layer_idx].astype(jnp.float32)).astype(jnp.bfloat16)
        query_part = jnp.dot(scaled, w_query[layer_idx], preferred_element_type=jnp.float32)
        key_part = jnp.dot(scaled, w_key[layer_idx], preferred_element_type=jnp.float32)
        value_part = jnp.dot(scaled, w_value[layer_idx], preferred_element_type=jnp.float32)
        squares = lax.psum(local_squares, "ctx")
        raw_query, raw_key, raw_value = lax.psum((query_part, key_part, value_part), "ctx")
        reciprocal_value = lax.rsqrt(squares / D + norm_eps)
        query = rotate(
            (raw_query * reciprocal_value[:, None]).reshape(seq_count, query_local, head_width),
            lengths,
        ).astype(jnp.bfloat16)
        fresh_lookup_vector = rotate(
            (raw_key * reciprocal_value[:, None]).reshape(seq_count, kv_local, head_width), lengths
        ).astype(jnp.bfloat16)
        new_value = (
            (raw_value * reciprocal_value[:, None])
            .reshape(seq_count, kv_local, head_width)
            .astype(jnp.bfloat16)
        )
        shared_head_sets = query.reshape(seq_count, kv_local, group_size, head_width)
        scores = (
            jnp.einsum(
                "bkgd,bksd->bkgs",
                shared_head_sets,
                key_cache[layer_idx],
                preferred_element_type=jnp.float32,
            )
            * logit_multiplier
        )
        masked = jnp.where(usable, scores, mask_fill)
        local_max = jnp.max(masked, axis=-1)
        attention_probabilities = jnp.where(usable, jnp.exp(masked - local_max[..., None]), 0.0)
        local_sum = jnp.sum(attention_probabilities, axis=-1)
        local_out = jnp.einsum(
            "bkgs,bksd->bkgd",
            attention_probabilities.astype(jnp.bfloat16),
            value_cache[layer_idx],
            preferred_element_type=jnp.float32,
        )
        largest, total_sum, total_out = merged(
            (local_max, local_sum, local_out), "ctx", combine_partial
        )
        self_match_logit = (
            jnp.einsum(
                "uryj,urj->ury",
                shared_head_sets,
                fresh_lookup_vector,
                preferred_element_type=jnp.float32,
            )
            * logit_multiplier
        )
        row_top = jnp.maximum(largest, self_match_logit)
        carried = jnp.exp(largest - row_top)
        fresh = jnp.exp(self_match_logit - row_top)
        fresh_rounded = lax.optimization_barrier(fresh.astype(jnp.bfloat16)).astype(jnp.float32)
        numerator = (
            total_out * carried[..., None]
            + fresh_rounded[..., None] * new_value.astype(jnp.float32)[:, :, None, :]
        )
        denominator = total_sum * carried + fresh
        context = (
            (numerator / denominator[..., None])
            .reshape(seq_count, query_local * head_width)
            .astype(jnp.bfloat16)
        )
        head_part = jnp.dot(context, w_out[layer_idx], preferred_element_type=jnp.float32)
        stream = stream + lax.psum(head_part, "tp")
    return stream


def solution(mesh):
    return jax.shard_map(
        shards,
        mesh=mesh,
        in_specs=(
            P(None, "ctx"),
            P(None, "ctx"),
            P(None, "ctx", "tp"),
            P(None, "ctx", "tp"),
            P(None, "ctx", "tp"),
            P(None, "tp", "ctx"),
            P(None, None, "tp", "ctx", None),
            P(None, None, "tp", "ctx", None),
            P(),
        ),
        out_specs=P(None, "ctx"),
        check_vma=False,
    )
```

profile of v0, /device:TPU:0, one launch (start us, length us, event | category | flops | bytes accessed | tf_op | source)
XLA Modules:
  0.0 526.2 jit_solution(14332039399861125533)
XLA Ops:
  6.5 0.9 slice_convert_fusion
  7.4 3.6 fusion.30
  11.3 0.2 fusion.65
  11.5 1.2 fusion.67
  12.7 25.5 %all-reduce.3 = (f32[8]{0:T(128)S(1)}, f32[8,256]{1,0:T(8,128)S(1)}, f32[8,256]{1,0:T(8,128)S(1)}) all-reduce(f32[8]{0:T(128)S(1)} %fusion.97, f32[8,256]{1,0:T(8,128)S(1)} %fusion.67, f32[8,256]{1,0:T(8,128)S(1)} %fusion.65), channel_id=1, replica_groups=mesh['ctx'=8,'tp'=4] {'ctx'}, use_global_device_ids=true, to_apply=%region_2.0 | all-reduce | flops 4104 | bytes 32832 | tf_op jit(solution)/shard_map/psum | solution.py:68
  38.7 28.5 %all-reduce.9.cloned.1.call-done = f32[8,2048]{1,0:T(8,128)} async-done(((f32[8,2048]{1,0:T(8,128)}), f32[8,2048]{1,0:T(8,128)}) %all-reduce.9.cloned.1.call-update) | async-done | bytes 65552 | tf_op jit(solution)/shard_map/psum | solution.py:69
  67.2 0.9 multiply_bitcast_fusion.3
  68.3 1.5 fusion.175
  69.8 1.4 fusion.69
  71.1 9.2 %all-gather.2 = f32[64,2,8,128]{3,2,1,0:T(8,128)S(1)} all-gather(f32[8,2,8,128]{3,2,1,0:T(8,128)S(1)} %fusion.69), channel_id=4, replica_groups=mesh['ctx'=8,'tp'=4] {'ctx'}, dimensions={0}, use_global_device_ids=true | all-gather | bytes 589824 | tf_op jit(solution)/shard_map/all_gather | solution.py:14
  80.4 0.2 fusion.89
  80.6 8.9 %all-gather.1 = f32[64,2,8]{2,1,0:T(2,128)S(1)} all-gather(f32[8,2,8]{2,1,0:T(2,128)S(1)} %fusion.89), channel_id=3, replica_groups=mesh['ctx'=8,'tp'=4] {'ctx'}, dimensions={0}, use_global_device_ids=true | all-gather | bytes 4608 | tf_op jit(solution)/shard_map/all_gather | solution.py:14
  89.5 8.6 %all-gather = f32[64,2,8]{2,1,0:T(2,128)S(1)} all-gather(f32[8,2,8]{2,1,0:T(2,128)S(1)} %get-tuple-element.397), channel_id=2, replica_groups=mesh['ctx'=8,'tp'=4] {'ctx'}, dimensions={0}, use_global_device_ids=true | all-gather | bytes 4608 | tf_op jit(solution)/shard_map/all_gather | solution.py:14
  98.1 1.4 while.56
  99.5 0.2 fusion.144
  99.9 2.8 fusion.28
  102.8 19.0 %psum.144 = f32[8,1024]{1,0:T(8,128)S(1)} all-reduce(f32[8,1024]{1,0:T(8,128)S(1)} %fusion.28), channel_id=1, replica_groups=mesh['ctx'=8,'tp'=4] {'tp'}, use_global_device_ids=true, to_apply=%region_9.10 | all-reduce | flops 8192 | bytes 65536 | tf_op jit(solution)/shard_map/psum | solution.py:130
  122.0 1.2 fusion.60
  123.3 3.5 fusion.26
  126.7 22.3 %all-reduce.2 = (f32[8]{0:T(128)S(1)}, f32[8,256]{1,0:T(8,128)S(1)}, f32[8,256]{1,0:T(8,128)S(1)}) all-reduce(f32[8]{0:T(128)S(1)} %get-tuple-element.361, f32[8,256]{1,0:T(8,128)S(1)} %fusion.60, f32[8,256]{1,0:T(8,128)S(1)} %fusion.58), channel_id=1, replica_groups=mesh['ctx'=8,'tp'=4] {'ctx'}, use_global_device_ids=true, to_apply=%region_12.13 | all-reduce | flops 4104 | bytes 32832 | tf_op jit(solution)/shard_map/psum | solution.py:68
  149.4 50.2 %all-reduce.11.cloned.1.call-done = f32[8,2048]{1,0:T(8,128)} async-done(((f32[8,2048]{1,0:T(8,128)}), f32[8,2048]{1,0:T(8,128)}) %all-reduce.11.cloned.1.call-update) | async-done | bytes 65552 | tf_op jit(solution)/shard_map/psum | solution.py:69
  199.6 0.9 multiply_bitcast_fusion.2
  200.6 1.5 fusion.176
  202.2 1.4 fusion.62
  203.5 9.2 %all-gather.5 = f32[64,2,8,128]{3,2,1,0:T(8,128)S(1)} all-gather(f32[8,2,8,128]{3,2,1,0:T(8,128)S(1)} %fusion.62), channel_id=7, replica_groups=mesh['ctx'=8,'tp'=4] {'ctx'}, dimensions={0}, use_global_device_ids=true | all-gather | bytes 589824 | tf_op jit(solution)/shard_map/all_gather | solution.py:14
  212.8 0.2 fusion.91
  213.0 8.9 %all-gather.4 = f32[64,2,8]{2,1,0:T(2,128)S(1)} all-gather(f32[8,2,8]{2,1,0:T(2,128)S(1)} %fusion.91), channel_id=6, replica_groups=mesh['ctx'=8,'tp'=4] {'ctx'}, dimensions={0}, use_global_device_ids=true | all-gather | bytes 4608 | tf_op jit(solution)/shard_map/all_gather | solution.py:14
  221.9 8.6 %all-gather.3 = f32[64,2,8]{2,1,0:T(2,128)S(1)} all-gather(f32[8,2,8]{2,1,0:T(2,128)S(1)} %get-tuple-element.399), channel_id=5, replica_groups=mesh['ctx'=8,'tp'=4] {'ctx'}, dimensions={0}, use_global_device_ids=true | all-gather | bytes 4608 | tf_op jit(solution)/shard_map/all_gather | solution.py:14
  230.5 0.2 fusion.142
  230.7 1.4 while.57
  232.3 2.8 fusion.24
  235.1 19.0 %psum.149 = f32[8,1024]{1,0:T(8,128)S(1)} all-reduce(f32[8,1024]{1,0:T(8,128)S(1)} %fusion.24), channel_id=1, replica_groups=mesh['ctx'=8,'tp'=4] {'tp'}, use_global_device_ids=true, to_apply=%region_19.20 | all-reduce | flops 8192 | bytes 65536 | tf_op jit(solution)/shard_map/psum | solution.py:130
  254.2 0.2 fusion.51
  254.4 1.2 fusion.53
  255.6 3.5 fusion.22
  259.1 22.3 %all-reduce.1 = (f32[8]{0:T(128)S(1)}, f32[8,256]{1,0:T(8,128)S(1)}, f32[8,256]{1,0:T(8,128)S(1)}) all-reduce(f32[8]{0:T(128)S(1)} %get-tuple-element.343, f32[8,256]{1,0:T(8,128)S(1)} %fusion.53, f32[8,256]{1,0:T(8,128)S(1)} %fusion.51), channel_id=1, replica_groups=mesh['ctx'=8,'tp'=4] {'ctx'}, use_global_device_ids=true, to_apply=%region_22.23 | all-reduce | flops 4104 | bytes 32832 | tf_op jit(solution)/shard_map/psum | solution.py:68
  281.8 50.2 %all-reduce.13.cloned.1.call-done = f32[8,2048]{1,0:T(8,128)} async-done(((f32[8,2048]{1,0:T(8,128)}), f32[8,2048]{1,0:T(8,128)}) %all-reduce.13.cloned.1.call-update) | async-done | bytes 65552 | tf_op jit(solution)/shard_map/psum | solution.py:69
  332.0 0.9 multiply_bitcast_fusion.1
  333.0 1.5 fusion.177
  334.5 1.4 fusion.55
  335.9 9.4 %all-gather.8 = f32[64,2,8,128]{3,2,1,0:T(8,128)S(1)} all-gather(f32[8,2,8,128]{3,2,1,0:T(8,128)S(1)} %fusion.55), channel_id=10, replica_groups=mesh['ctx'=8,'tp'=4] {'ctx'}, dimensions={0}, use_global_device_ids=true | all-gather | bytes 589824 | tf_op jit(solution)/shard_map/all_gather | solution.py:14
  345.3 0.2 fusion.93
  345.5 8.9 %all-gather.7 = f32[64,2,8]{2,1,0:T(2,128)S(1)} all-gather(f32[8,2,8]{2,1,0:T(2,128)S(1)} %fusion.93), channel_id=9, replica_groups=mesh['ctx'=8,'tp'=4] {'ctx'}, dimensions={0}, use_global_device_ids=true | all-gather | bytes 4608 | tf_op jit(solution)/shard_map/all_gather | solution.py:14
  354.4 8.6 %all-gather.6 = f32[64,2,8]{2,1,0:T(2,128)S(1)} all-gather(f32[8,2,8]{2,1,0:T(2,128)S(1)} %get-tuple-element.401), channel_id=8, replica_groups=mesh['ctx'=8,'tp'=4] {'ctx'}, dimensions={0}, use_global_device_ids=true | all-gather | bytes 4608 | tf_op jit(solution)/shard_map/all_gather | solution.py:14
  363.0 0.2 fusion.140
  363.2 1.4 while.58
  364.8 2.8 fusion.20
  367.7 19.0 %psum.154 = f32[8,1024]{1,0:T(8,128)S(1)} all-reduce(f32[8,1024]{1,0:T(8,128)S(1)} %fusion.20), channel_id=1, replica_groups=mesh['ctx'=8,'tp'=4] {'tp'}, use_global_device_ids=true, to_apply=%region_29.30 | all-reduce | flops 8192 | bytes 65536 | tf_op jit(solution)/shard_map/psum | solution.py:130
  387.0 1.2 fusion.46
  388.2 3.5 fusion.18
  391.7 22.3 %all-reduce = (f32[8]{0:T(128)S(1)}, f32[8,256]{1,0:T(8,128)S(1)}, f32[8,256]{1,0:T(8,128)S(1)}) all-reduce(f32[8]{0:T(128)S(1)} %get-tuple-element.341, f32[8,256]{1,0:T(8,128)S(1)} %fusion.46, f32[8,256]{1,0:T(8,128)S(1)} %fusion.44), channel_id=1, replica_groups=mesh['ctx'=8,'tp'=4] {'ctx'}, use_global_device_ids=true, to_apply=%region_32.33 | all-reduce | flops 4104 | bytes 32832 | tf_op jit(solution)/shard_map/psum | solution.py:68
  414.3 50.2 %all-reduce.15.cloned.1.call-done = f32[8,2048]{1,0:T(8,128)} async-done(((f32[8,2048]{1,0:T(8,128)}), f32[8,2048]{1,0:T(8,128)}) %all-reduce.15.cloned.1.call-update) | async-done | bytes 65552 | tf_op jit(solution)/shard_map/psum | solution.py:69
  464.5 0.9 multiply_bitcast_fusion
  465.5 1.5 fusion.178
  467.1 1.4 fusion.48
  468.4 9.2 %all-gather.11 = f32[64,2,8,128]{3,2,1,0:T(8,128)S(1)} all-gather(f32[8,2,8,128]{3,2,1,0:T(8,128)S(1)} %fusion.48), channel_id=13, replica_groups=mesh['ctx'=8,'tp'=4] {'ctx'}, dimensions={0}, use_global_device_ids=true | all-gather | bytes 589824 | tf_op jit(solution)/shard_map/all_gather | solution.py:14
  477.7 0.2 fusion.95
  477.9 8.9 %all-gather.10 = f32[64,2,8]{2,1,0:T(2,128)S(1)} all-gather(f32[8,2,8]{2,1,0:T(2,128)S(1)} %fusion.95), channel_id=12, replica_groups=mesh['ctx'=8,'tp'=4] {'ctx'}, dimensions={0}, use_global_device_ids=true | all-gather | bytes 4608 | tf_op jit(solution)/shard_map/all_gather | solution.py:14
  486.8 8.6 %all-gather.9 = f32[64,2,8]{2,1,0:T(2,128)S(1)} all-gather(f32[8,2,8]{2,1,0:T(2,128)S(1)} %get-tuple-element.403), channel_id=11, replica_groups=mesh['ctx'=8,'tp'=4] {'ctx'}, dimensions={0}, use_global_device_ids=true | all-gather | bytes 4608 | tf_op jit(solution)/shard_map/all_gather | solution.py:14
  495.4 0.2 fusion.138
  495.6 1.4 while.59
  497.2 2.8 fusion.16
  500.0 19.0 %psum.159 = f32[8,1024]{1,0:T(8,128)S(1)} all-reduce(f32[8,1024]{1,0:T(8,128)S(1)} %fusion.16), channel_id=1, replica_groups=mesh['ctx'=8,'tp'=4] {'tp'}, use_global_device_ids=true, to_apply=%region_39.40 | all-reduce | flops 8192 | bytes 65536 | tf_op jit(solution)/shard_map/psum | solution.py:130
  519.0 0.6 add.183
  (250 shorter events, 7.6 us)
Async XLA Ops:
  6.5 60.7 %all-reduce.9.cloned.1.call-start = ((), (), s32[]{:S(2)}) async-start(), calls=%async_computation | async-start | bytes 131072 | tf_op jit(solution)/shard_map/psum | solution.py:69
  7.4 3.7 copy-start.1
  7.4 3.9 copy-start
  7.4 30.8 %copy-start.2 = (s32[8]{0:T(128)S(1)}, s32[8]{0:T(128)}, u32[]{:S(2)}) copy-start(s32[8]{0:T(128)} %param.25) | copy-start | bytes 100
  11.1 188.5 %all-reduce.11.cloned.1.call-start = ((), (), s32[]{:S(2)}) async-start(), calls=%async_computation.1 | async-start | bytes 131072 | tf_op jit(solution)/shard_map/psum | solution.py:69
  149.3 182.7 %all-reduce.13.cloned.1.call-start = ((), (), s32[]{:S(2)}) async-start(), calls=%async_computation.2 | async-start | bytes 131072 | tf_op jit(solution)/shard_map/psum | solution.py:69
  281.6 182.9 %all-reduce.15.cloned.1.call-start = ((), (), s32[]{:S(2)}) async-start(), calls=%async_computation.3 | async-start | bytes 131072 | tf_op jit(solution)/shard_map/psum | solution.py:69
Sparse Core Ops, SparseCore 0:
  11.2 55.9 all-reduce.8
  149.4 50.1 all-reduce.10
  281.8 50.1 all-reduce.12
  414.3 50.1 all-reduce.14
where the time goes:
time: 528 us; the launch traced here: 526 us
  blocking collectives  275 us (52%)
  waiting for transfers between devices  179 us (34%)
  matrix products  43.4 us (8%)
  between operations  13.6 us (3%)
  other arithmetic  12 us (2%)
    psum x4, waiting for transfers between devices, shards(): lax.psum((query_part, key_part, value_part), 'ctx')  179 us
    all_gather x12, blocking collectives, merged(): pieces = jax.tree.map(lambda part: lax.all_gather(part, axis), value)  107 us
    psum x4, blocking collectives, shards(): squares = lax.psum(local_squares, 'ctx')  92.6 us
    psum x4, blocking collectives, shards(): stream = stream + lax.psum(head_part, 'tp')  75.9 us
    dot_general x4, matrix products, shards(): jnp.dot(scaled, w_query[layer_idx], preferred_element_type=jnp.float32)  14 us
    dot_general x4, matrix products, shards(): jnp.dot(context, w_out[layer_idx], preferred_element_type=jnp.float32)  11.4 us
  transfers between devices with their start and end apart: 4, of which 4 were waited for; matrix products, arithmetic and copies ran while one was open for 0% of the time, Pallas kernels for 0%

commit v1 on v0

--- a/solution.py
+++ b/solution.py
@@ -127,7 +127,7 @@
             .astype(jnp.bfloat16)
         )
         head_part = jnp.dot(context, w_out[layer_idx], preferred_element_type=jnp.float32)
-        stream = stream + lax.psum(head_part, "tp")
+        stream = stream + jnp.sum(lax.all_gather(head_part, "tp"), axis=0)
     return stream
 
 

time: 528 us -> 514 us (0.973)
  blocking collectives: 275 us -> 254 us
  waiting for transfers between devices: 179 us -> 188 us
    psum x4 -> x0, blocking collectives: 75.9 us -> none  [shards(): stream = stream + lax.psum(head_part, 'tp')]
    all_gather x0 -> x4, blocking collectives: none -> 53.9 us  [shards(): stream = stream + jnp.sum(lax.all_gather(head_part, 'tp'), axis=0)]
    psum x4, waiting for transfers between devices: 179 us -> 187 us  [shards(): lax.psum((query_part, key_part, value_part), 'ctx')]
where the time goes in v1:
time: 514 us; the launch traced here: 513 us
  blocking collectives  254 us (49%)
  waiting for transfers between devices  188 us (37%)
  matrix products  43.4 us (8%)
  between operations  13.6 us (3%)
  other arithmetic  12 us (2%)
    psum x4, waiting for transfers between devices, shards(): lax.psum((query_part, key_part, value_part), 'ctx')  187 us
    all_gather x12, blocking collectives, merged(): pieces = jax.tree.map(lambda part: lax.all_gather(part, axis), value)  107 us
    psum x4, blocking collectives, shards(): squares = lax.psum(local_squares, 'ctx')  92.6 us
    all_gather x4, blocking collectives, shards(): stream = stream + jnp.sum(lax.all_gather(head_part, 'tp'), axis=0)  53.9 us
    dot_general x4, matrix products, shards(): jnp.dot(scaled, w_query[layer_idx], preferred_element_type=jnp.float32)  14 us
    dot_general x4, matrix products, shards(): jnp.dot(context, w_out[layer_idx], preferred_element_type=jnp.float32)  11.4 us
  transfers between devices with their start and end apart: 4, of which 4 were waited for; matrix products, arithmetic and copies ran while one was open for 0% of the time, Pallas kernels for 0%

profile of v1, /device:TPU:0, one launch (start us, length us, event | category | flops | bytes accessed | tf_op | source)
XLA Modules:
  0.0 512.6 jit_solution(9293213684351406145)
XLA Ops:
  6.5 0.9 slice_convert_fusion
  7.4 3.6 fusion.30
  11.3 0.2 fusion.65
  11.5 1.2 fusion.67
  12.7 25.5 %all-reduce.3 = (f32[8]{0:T(128)S(1)}, f32[8,256]{1,0:T(8,128)S(1)}, f32[8,256]{1,0:T(8,128)S(1)}) all-reduce(f32[8]{0:T(128)S(1)} %fusion.97, f32[8,256]{1,0:T(8,128)S(1)} %fusion.67, f32[8,256]{1,0:T(8,128)S(1)} %fusion.65), channel_id=1, replica_groups=mesh['ctx'=8,'tp'=4] {'ctx'}, use_global_device_ids=true, to_apply=%region_2.0 | all-reduce | flops 4104 | bytes 32832 | tf_op jit(solution)/shard_map/psum | solution.py:68
  38.7 28.5 %all-reduce.9.cloned.1.call-done = f32[8,2048]{1,0:T(8,128)} async-done(((f32[8,2048]{1,0:T(8,128)}), f32[8,2048]{1,0:T(8,128)}) %all-reduce.9.cloned.1.call-update) | async-done | bytes 65552 | tf_op jit(solution)/shard_map/psum | solution.py:69
  67.2 0.9 multiply_bitcast_fusion.3
  68.3 1.5 fusion.175
  69.8 1.4 fusion.69
  71.1 9.2 %all-gather.2 = f32[64,2,8,128]{3,2,1,0:T(8,128)S(1)} all-gather(f32[8,2,8,128]{3,2,1,0:T(8,128)S(1)} %fusion.69), channel_id=4, replica_groups=mesh['ctx'=8,'tp'=4] {'ctx'}, dimensions={0}, use_global_device_ids=true | all-gather | bytes 589824 | tf_op jit(solution)/shard_map/all_gather | solution.py:14
  80.4 0.2 fusion.89
  80.6 8.9 %all-gather.1 = f32[64,2,8]{2,1,0:T(2,128)S(1)} all-gather(f32[8,2,8]{2,1,0:T(2,128)S(1)} %fusion.89), channel_id=3, replica_groups=mesh['ctx'=8,'tp'=4] {'ctx'}, dimensions={0}, use_global_device_ids=true | all-gather | bytes 4608 | tf_op jit(solution)/shard_map/all_gather | solution.py:14
  89.5 8.6 %all-gather = f32[64,2,8]{2,1,0:T(2,128)S(1)} all-gather(f32[8,2,8]{2,1,0:T(2,128)S(1)} %get-tuple-element.397), channel_id=2, replica_groups=mesh['ctx'=8,'tp'=4] {'ctx'}, dimensions={0}, use_global_device_ids=true | all-gather | bytes 4608 | tf_op jit(solution)/shard_map/all_gather | solution.py:14
  98.1 1.4 while.56
  99.5 0.2 fusion.144
  99.9 2.8 fusion.28
  102.8 13.5 %all-gather.3 = f32[32,1024]{1,0:T(8,128)S(1)} all-gather(f32[8,1024]{1,0:T(8,128)S(1)} %fusion.28), channel_id=5, replica_groups=mesh['ctx'=8,'tp'=4] {'tp'}, dimensions={0}, use_global_device_ids=true | all-gather | bytes 163840 | tf_op jit(solution)/shard_map/all_gather | solution.py:130
  116.6 1.2 fusion.60
  117.8 3.5 fusion.26
  121.3 22.3 %all-reduce.2 = (f32[8]{0:T(128)S(1)}, f32[8,256]{1,0:T(8,128)S(1)}, f32[8,256]{1,0:T(8,128)S(1)}) all-reduce(f32[8]{0:T(128)S(1)} %get-tuple-element.361, f32[8,256]{1,0:T(8,128)S(1)} %fusion.60, f32[8,256]{1,0:T(8,128)S(1)} %fusion.58), channel_id=1, replica_groups=mesh['ctx'=8,'tp'=4] {'ctx'}, use_global_device_ids=true, to_apply=%region_12.13 | all-reduce | flops 4104 | bytes 32832 | tf_op jit(solution)/shard_map/psum | solution.py:68
  143.9 53.0 %all-reduce.11.cloned.1.call-done = f32[8,2048]{1,0:T(8,128)} async-done(((f32[8,2048]{1,0:T(8,128)}), f32[8,2048]{1,0:T(8,128)}) %all-reduce.11.cloned.1.call-update) | async-done | bytes 65552 | tf_op jit(solution)/shard_map/psum | solution.py:69
  196.9 0.9 multiply_bitcast_fusion.2
  197.9 1.5 fusion.176
  199.5 1.4 fusion.62
  200.8 9.2 %all-gather.6 = f32[64,2,8,128]{3,2,1,0:T(8,128)S(1)} all-gather(f32[8,2,8,128]{3,2,1,0:T(8,128)S(1)} %fusion.62), channel_id=8, replica_groups=mesh['ctx'=8,'tp'=4] {'ctx'}, dimensions={0}, use_global_device_ids=true | all-gather | bytes 589824 | tf_op jit(solution)/shard_map/all_gather | solution.py:14
  210.1 0.2 fusion.91
  210.3 8.9 %all-gather.5 = f32[64,2,8]{2,1,0:T(2,128)S(1)} all-gather(f32[8,2,8]{2,1,0:T(2,128)S(1)} %fusion.91), channel_id=7, replica_groups=mesh['ctx'=8,'tp'=4] {'ctx'}, dimensions={0}, use_global_device_ids=true | all-gather | bytes 4608 | tf_op jit(solution)/shard_map/all_gather | solution.py:14
  219.2 8.6 %all-gather.4 = f32[64,2,8]{2,1,0:T(2,128)S(1)} all-gather(f32[8,2,8]{2,1,0:T(2,128)S(1)} %get-tuple-element.399), channel_id=6, replica_groups=mesh['ctx'=8,'tp'=4] {'ctx'}, dimensions={0}, use_global_device_ids=true | all-gather | bytes 4608 | tf_op jit(solution)/shard_map/all_gather | solution.py:14
  227.8 0.2 fusion.142
  228.0 1.4 while.57
  229.6 2.8 fusion.24
  232.4 13.5 %all-gather.7 = f32[32,1024]{1,0:T(8,128)S(1)} all-gather(f32[8,1024]{1,0:T(8,128)S(1)} %fusion.24), channel_id=9, replica_groups=mesh['ctx'=8,'tp'=4] {'tp'}, dimensions={0}, use_global_device_ids=true | all-gather | bytes 163840 | tf_op jit(solution)/shard_map/all_gather | solution.py:130
  246.1 0.2 fusion.51
  246.2 1.2 fusion.53
  247.5 3.5 fusion.22
  250.9 22.3 %all-reduce.1 = (f32[8]{0:T(128)S(1)}, f32[8,256]{1,0:T(8,128)S(1)}, f32[8,256]{1,0:T(8,128)S(1)}) all-reduce(f32[8]{0:T(128)S(1)} %get-tuple-element.343, f32[8,256]{1,0:T(8,128)S(1)} %fusion.53, f32[8,256]{1,0:T(8,128)S(1)} %fusion.51), channel_id=1, replica_groups=mesh['ctx'=8,'tp'=4] {'ctx'}, use_global_device_ids=true, to_apply=%region_22.23 | all-reduce | flops 4104 | bytes 32832 | tf_op jit(solution)/shard_map/psum | solution.py:68
  273.6 53.0 %all-reduce.13.cloned.1.call-done = f32[8,2048]{1,0:T(8,128)} async-done(((f32[8,2048]{1,0:T(8,128)}), f32[8,2048]{1,0:T(8,128)}) %all-reduce.13.cloned.1.call-update) | async-done | bytes 65552 | tf_op jit(solution)/shard_map/psum | solution.py:69
  326.6 0.9 multiply_bitcast_fusion.1
  327.6 1.5 fusion.177
  329.1 1.4 fusion.55
  330.5 9.4 %all-gather.10 = f32[64,2,8,128]{3,2,1,0:T(8,128)S(1)} all-gather(f32[8,2,8,128]{3,2,1,0:T(8,128)S(1)} %fusion.55), channel_id=12, replica_groups=mesh['ctx'=8,'tp'=4] {'ctx'}, dimensions={0}, use_global_device_ids=true | all-gather | bytes 589824 | tf_op jit(solution)/shard_map/all_gather | solution.py:14
  339.9 0.2 fusion.93
  340.1 8.9 %all-gather.9 = f32[64,2,8]{2,1,0:T(2,128)S(1)} all-gather(f32[8,2,8]{2,1,0:T(2,128)S(1)} %fusion.93), channel_id=11, replica_groups=mesh['ctx'=8,'tp'=4] {'ctx'}, dimensions={0}, use_global_device_ids=true | all-gather | bytes 4608 | tf_op jit(solution)/shard_map/all_gather | solution.py:14
  349.0 8.6 %all-gather.8 = f32[64,2,8]{2,1,0:T(2,128)S(1)} all-gather(f32[8,2,8]{2,1,0:T(2,128)S(1)} %get-tuple-element.401), channel_id=10, replica_groups=mesh['ctx'=8,'tp'=4] {'ctx'}, dimensions={0}, use_global_device_ids=true | all-gather | bytes 4608 | tf_op jit(solution)/shard_map/all_gather | solution.py:14
  357.6 0.2 fusion.140
  357.8 1.4 while.58
  359.4 2.8 fusion.20
  362.3 13.5 %all-gather.11 = f32[32,1024]{1,0:T(8,128)S(1)} all-gather(f32[8,1024]{1,0:T(8,128)S(1)} %fusion.20), channel_id=13, replica_groups=mesh['ctx'=8,'tp'=4] {'tp'}, dimensions={0}, use_global_device_ids=true | all-gather | bytes 163840 | tf_op jit(solution)/shard_map/all_gather | solution.py:130
  376.1 1.2 fusion.46
  377.3 3.5 fusion.18
  380.8 22.3 %all-reduce = (f32[8]{0:T(128)S(1)}, f32[8,256]{1,0:T(8,128)S(1)}, f32[8,256]{1,0:T(8,128)S(1)}) all-reduce(f32[8]{0:T(128)S(1)} %get-tuple-element.341, f32[8,256]{1,0:T(8,128)S(1)} %fusion.46, f32[8,256]{1,0:T(8,128)S(1)} %fusion.44), channel_id=1, replica_groups=mesh['ctx'=8,'tp'=4] {'ctx'}, use_global_device_ids=true, to_apply=%region_32.33 | all-reduce | flops 4104 | bytes 32832 | tf_op jit(solution)/shard_map/psum | solution.py:68
  403.4 53.0 %all-reduce.15.cloned.1.call-done = f32[8,2048]{1,0:T(8,128)} async-done(((f32[8,2048]{1,0:T(8,128)}), f32[8,2048]{1,0:T(8,128)}) %all-reduce.15.cloned.1.call-update) | async-done | bytes 65552 | tf_op jit(solution)/shard_map/psum | solution.py:69
  456.4 0.9 multiply_bitcast_fusion
  457.4 1.5 fusion.178
  459.0 1.4 fusion.48
  460.3 9.2 %all-gather.14 = f32[64,2,8,128]{3,2,1,0:T(8,128)S(1)} all-gather(f32[8,2,8,128]{3,2,1,0:T(8,128)S(1)} %fusion.48), channel_id=16, replica_groups=mesh['ctx'=8,'tp'=4] {'ctx'}, dimensions={0}, use_global_device_ids=true | all-gather | bytes 589824 | tf_op jit(solution)/shard_map/all_gather | solution.py:14
  469.6 0.2 fusion.95
  469.8 8.9 %all-gather.13 = f32[64,2,8]{2,1,0:T(2,128)S(1)} all-gather(f32[8,2,8]{2,1,0:T(2,128)S(1)} %fusion.95), channel_id=15, replica_groups=mesh['ctx'=8,'tp'=4] {'ctx'}, dimensions={0}, use_global_device_ids=true | all-gather | bytes 4608 | tf_op jit(solution)/shard_map/all_gather | solution.py:14
  478.7 8.6 %all-gather.12 = f32[64,2,8]{2,1,0:T(2,128)S(1)} all-gather(f32[8,2,8]{2,1,0:T(2,128)S(1)} %get-tuple-element.403), channel_id=14, replica_groups=mesh['ctx'=8,'tp'=4] {'ctx'}, dimensions={0}, use_global_device_ids=true | all-gather | bytes 4608 | tf_op jit(solution)/shard_map/all_gather | solution.py:14
  487.3 0.2 fusion.138
  487.5 1.4 while.59
  489.1 2.8 fusion.16
  491.9 13.5 %all-gather.15 = f32[32,1024]{1,0:T(8,128)S(1)} all-gather(f32[8,1024]{1,0:T(8,128)S(1)} %fusion.16), channel_id=17, replica_groups=mesh['ctx'=8,'tp'=4] {'tp'}, dimensions={0}, use_global_device_ids=true | all-gather | bytes 163840 | tf_op jit(solution)/shard_map/all_gather | solution.py:130
  505.4 0.6 add.175
  (254 shorter events, 7.7 us)
Async XLA Ops:
  6.5 60.7 %all-reduce.9.cloned.1.call-start = ((), (), s32[]{:S(2)}) async-start(), calls=%async_computation | async-start | bytes 131072 | tf_op jit(solution)/shard_map/psum | solution.py:69
  7.4 3.7 copy-start.1
  7.4 3.9 copy-start
  7.4 30.8 %copy-start.2 = (s32[8]{0:T(128)S(1)}, s32[8]{0:T(128)}, u32[]{:S(2)}) copy-start(s32[8]{0:T(128)} %param.25) | copy-start | bytes 100
  11.1 185.8 %all-reduce.11.cloned.1.call-start = ((), (), s32[]{:S(2)}) async-start(), calls=%async_computation.1 | async-start | bytes 131072 | tf_op jit(solution)/shard_map/psum | solution.py:69
  143.8 182.8 %all-reduce.13.cloned.1.call-start = ((), (), s32[]{:S(2)}) async-start(), calls=%async_computation.2 | async-start | bytes 131072 | tf_op jit(solution)/shard_map/psum | solution.py:69
  273.5 182.9 %all-reduce.15.cloned.1.call-start = ((), (), s32[]{:S(2)}) async-start(), calls=%async_computation.3 | async-start | bytes 131072 | tf_op jit(solution)/shard_map/psum | solution.py:69
Sparse Core Ops, SparseCore 0:
  11.2 55.9 all-reduce.8
  143.9 52.9 all-reduce.10
  273.6 52.9 all-reduce.12
  403.4 52.9 all-reduce.14
